TPU v7x, 128 devices: a whole 4x4x4 slice. The times are simulated.
128 devices in a mesh: data: 128 (over z, y, x, core).
Axes of the slice: x: 4, y: 4, z: 4, core: 2. Of those that a mesh axis runs over, the one named last changes fastest.
Arguments:
- act_in: bfloat16 [131072, 768], P('data')
- grad_out: bfloat16 [131072, 768], P('data')
- w_up: bfloat16 [2, 768, 3072], replicated
- w_down: bfloat16 [2, 3072, 768], replicated
- master_up: float32 [2, 768, 3072], P(None, 'data')
- master_down: float32 [2, 3072, 768], P(None, 'data')
- exp_avg_up: float32 [2, 768, 3072], P(None, 'data')
- exp_avg_down: float32 [2, 3072, 768], P(None, 'data')
- exp_sq_up: float32 [2, 768, 3072], P(None, 'data')
- exp_sq_down: float32 [2, 3072, 768], P(None, 'data')
- learn_rate: float32 [], replicated
- clip_norm: float32 [], replicated
Outputs:
- output 1: bfloat16 [2, 768, 3072], replicated
- output 2: bfloat16 [2, 3072, 768], replicated
- output 3: float32 [2, 768, 3072], P(None, 'data')
- output 4: float32 [2, 3072, 768], P(None, 'data')
- output 5: float32 [2, 768, 3072], P(None, 'data')
- output 6: float32 [2, 3072, 768], P(None, 'data')
- output 7: float32 [2, 768, 3072], P(None, 'data')
- output 8: float32 [2, 3072, 768], P(None, 'data')
- output 9: float32 [], replicated
All inputs are finite; a program needn't handle non-finite values.
Results may differ from a plain program's by a relative error of at most 0.00398.
Values are sent between devices in bfloat16 or wider.
A program may use at most 1 GiB of HBM per device.

v0:
```python
import jax
import jax.numpy as jnp
from jax import lax
from jax.sharding import PartitionSpec as P

STEP = 10
BETA_ONE = 0.9
BETA_TWO = 0.95
ADAM_EPS = 1e-8
NORM_EPS = 1e-6
INV_SQRT_TWO = 0.7071067811865476
INV_SQRT_TWO_PI = 0.3989422804014327


def gelu_parts(pre_act):
    normal_cdf = 0.5 * (1.0 + lax.erf(pre_act * INV_SQRT_TWO))
    normal_pdf = jnp.exp(-0.5 * pre_act * pre_act) * INV_SQRT_TWO_PI
    return pre_act * normal_cdf, normal_cdf + pre_act * normal_pdf


def local_grads(act_in, grad_out, w_up, w_down):
    z_one = jnp.einsum("td,df->tf", act_in, w_up[0], preferred_element_type=jnp.float32)
    gelu_one, slope_one = gelu_parts(z_one)
    act_one = gelu_one.astype(jnp.bfloat16)
    hidden = jnp.einsum("tf,fd->td", act_one, w_down[0], preferred_element_type=jnp.float32).astype(jnp.bfloat16)
    z_three = jnp.einsum("td,df->tf", hidden, w_up[1], preferred_element_type=jnp.float32)
    gelu_three, slope_three = gelu_parts(z_three)
    act_three = gelu_three.astype(jnp.bfloat16)
    g_four = jnp.einsum("tf,td->fd", act_three, grad_out, preferred_element_type=jnp.float32)
    dz_three = (jnp.einsum("td,fd->tf", grad_out, w_down[1], preferred_element_type=jnp.float32) * slope_three).astype(jnp.bfloat16)
    g_three = jnp.einsum("td,tf->df", hidden, dz_three, preferred_element_type=jnp.float32)
    d_hidden = jnp.einsum("tf,df->td", dz_three, w_up[1], preferred_element_type=jnp.float32).astype(jnp.bfloat16)
    g_two = jnp.einsum("tf,td->fd", act_one, d_hidden, preferred_element_type=jnp.float32)
    dz_one = (jnp.einsum("td,fd->tf", d_hidden, w_down[0], preferred_element_type=jnp.float32) * slope_one).astype(jnp.bfloat16)
    g_one = jnp.einsum("td,tf->df", act_in, dz_one, preferred_element_type=jnp.float32)
    return g_one, g_two, g_three, g_four


def adam_direction(exp_avg, exp_sq, grad, clip_scale):
    bias_one = 1.0 - BETA_ONE ** STEP
    bias_two = 1.0 - BETA_TWO ** STEP
    avg_new = BETA_ONE * exp_avg + (1.0 - BETA_ONE) * clip_scale * grad
    sq_new = BETA_TWO * exp_sq + (1.0 - BETA_TWO) * (clip_scale * clip_scale) * (grad * grad)
    direction = (avg_new / bias_one) / (jnp.sqrt(sq_new / bias_two) + ADAM_EPS)
    return avg_new, sq_new, direction


def sum_squares(stacked):
    return jnp.sum(stacked * stacked, axis=(1, 2))


def solution(mesh):
    group_size = mesh.shape["data"]
    batch_rows = P("data", None)
    state_rows = P(None, "data", None)
    replicated = P()

    def reduce_rows(grad):
        return lax.psum_scatter(grad, "data", scatter_dimension=0, tiled=True) / group_size

    def device_step(act_in, grad_out, w_up, w_down, master_up, master_down, exp_avg_up, exp_avg_down, exp_sq_up, exp_sq_down, learn_rate, clip_norm):
        g_one, g_two, g_three, g_four = local_grads(act_in, grad_out, w_up, w_down)
        shard_four = reduce_rows(g_four)
        shard_three = reduce_rows(g_three)
        shard_two = reduce_rows(g_two)
        shard_one = reduce_rows(g_one)
        grad_up = jnp.stack([shard_one, shard_three])
        grad_down = jnp.stack([shard_two, shard_four])
        local_sq = jnp.sum(grad_up * grad_up) + jnp.sum(grad_down * grad_down)
        grad_norm = jnp.sqrt(lax.psum(local_sq, "data"))
        clip_scale = jnp.minimum(1.0, clip_norm / (grad_norm + NORM_EPS))
        avg_up, sq_up, dir_up = adam_direction(exp_avg_up, exp_sq_up, grad_up, clip_scale)
        avg_down, sq_down, dir_down = adam_direction(exp_avg_down, exp_sq_down, grad_down, clip_scale)
        local_stats = jnp.concatenate([sum_squares(master_up), sum_squares(master_down), sum_squares(dir_up), sum_squares(dir_down)])
        norm_stats = lax.psum(local_stats, "data")
        trust_ratio = jnp.sqrt(norm_stats[0:4]) / jnp.sqrt(norm_stats[4:8])
        master_up_out = master_up - learn_rate * trust_ratio[0:2, None, None] * dir_up
        master_down_out = master_down - learn_rate * trust_ratio[2:4, None, None] * dir_down
        new_w_up = lax.all_gather(master_up_out.astype(jnp.bfloat16), "data", axis=1, tiled=True)
        new_w_down = lax.all_gather(master_down_out.astype(jnp.bfloat16), "data", axis=1, tiled=True)
        return (new_w_up, new_w_down, master_up_out, master_down_out, avg_up, avg_down, sq_up, sq_down, grad_norm)

    return jax.shard_map(device_step, mesh=mesh, in_specs=(batch_rows, batch_rows, replicated, replicated, state_rows, state_rows, state_rows, state_rows, state_rows, state_rows, replicated, replicated), out_specs=(replicated, replicated, state_rows, state_rows, state_rows, state_rows, state_rows, state_rows, replicated), check_vma=False)
```

profile of v0, /device:TPU:1, one launch (start us, length us, event | category | flops | bytes accessed | tf_op | source)
XLA Modules:
  0.0 1029.5 jit_solution(17850893650197578262)
XLA Ops:
  7.2 1.4 copy-done
  8.6 12.7 %multiply_convert_fusion.1 = (bf16[1024,3072]{1,0:T(8,128)(2,1)S(1)}, f32[1024,3072]{1,0:T(8,128)}) fusion(bf16[1024,768]{1,0:T(8,128)(2,1)S(1)} %copy-done, bf16[2,768,3072]{2,1,0:T(8,128)(2,1)} %param.14), kind=kOutput, calls=%fused_computation.16 | convolution fusion | flops 4847566848 | bytes 25165824 | tf_op jit(solution)/shard_map/td,df->tf/dot_general | solution.py:22
  21.3 5.0 fusion.29
  26.4 8.0 fusion.15
  34.4 12.2 %fusion.5 = bf16[1024,3072]{1,0:T(8,128)(2,1)S(1)} fusion(f32[1024,3072]{1,0:T(8,128)} %fusion.15, bf16[1024,768]{1,0:T(8,128)(2,1)S(1)} %copy-done.7, bf16[2,3072,768]{2,1,0:T(8,128)(2,1)S(1)} %copy-done.6), kind=kOutput, calls=%fused_computation.7 | convolution fusion | flops 4863295488 | bytes 25165824 | tf_op jit(solution)/shard_map/td,fd->tf/dot_general | solution.py:30
  46.5 6.3 fusion.32
  52.8 7.7 fusion.43
  60.5 18.0 %convolution_bitcast_fusion = f32[768,3072]{0,1:T(8,128)} fusion(bf16[1024,768]{1,0:T(8,128)(2,1)S(1)} %copy-done, f32[1024,3072]{1,0:T(8,128)} %get-tuple-element.43, bf16[1024,768]{1,0:T(8,128)(2,1)} %fusion.32, bf16[2,3072,768]{2,1,0:T(8,128)(2,1)} %param.15), kind=kOutput, calls=%fused_computation.19 | convolution fusion | flops 9695133696 | bytes 29884416 | tf_op jit(solution)/shard_map/td,tf->df/dot_general | solution.py:35
  78.6 11.1 %fusion.12 = f32[3072,768]{1,0:T(8,128)} fusion(bf16[1024,768]{1,0:T(8,128)(2,1)S(1)} %copy-done.7, f32[1024,3072]{1,0:T(8,128)} %fusion.15), kind=kOutput, calls=%fused_computation.18 | convolution fusion | flops 4847566848 | bytes 23592960 | tf_op jit(solution)/shard_map/tf,td->fd/dot_general | solution.py:29
  89.8 1.3 copy-done.9
  91.1 10.2 fusion.44
  101.5 0.8 copy-done.5
  102.7 198.4 %all-reduce.5.cloned.1.call-done = (f32[768,3072]{0,1:T(8,128)}, f32[768,3072]{0,1:T(8,128)}) async-done(((f32[768,3072]{0,1:T(8,128)}, f32[768,3072]{0,1:T(8,128)}), (f32[768,3072]{0,1:T(8,128)}, f32[768,3072]{0,1:T(8,128)})) %all-reduce.5.cloned.1.call-update) | async-done | bytes 18874384
  301.0 3.7 fusion.35
  304.8 0.5 copy.33
  305.2 0.5 copy.32
  305.7 0.8 multiply_reduce_fusion.5
  306.5 212.6 %reduce-scatter.7.cloned.1.call-done = f32[24,768]{1,0:T(8,128)} async-done(((f32[3072,768]{1,0:T(8,128)}), f32[24,768]{1,0:T(8,128)}) %reduce-scatter.7.cloned.1.call-update) | async-done | bytes 73744 | tf_op jit(solution)/shard_map/reduce_scatter | solution.py:59
  519.1 0.9 multiply_bitcast_fusion
  520.0 218.7 %reduce-scatter.5.cloned.1.call-done = f32[24,768]{1,0:T(8,128)} async-done(((f32[3072,768]{1,0:T(8,128)}), f32[24,768]{1,0:T(8,128)}) %reduce-scatter.5.cloned.1.call-update) | async-done | bytes 73744 | tf_op jit(solution)/shard_map/reduce_scatter | solution.py:59
  738.7 0.9 multiply_bitcast_fusion.1
  739.6 0.6 multiply_reduce_fusion.4
  742.1 64.3 %psum.14 = f32[]{:T(128)} all-reduce(f32[]{:T(128)S(6)} %add.58), channel_id=1, replica_groups=mesh['data'=128] {'data'}, use_global_device_ids=true, to_apply=%region_8.0 | all-reduce | flops 1 | bytes 8 | tf_op jit(solution)/shard_map/psum | solution.py:70
  807.2 1.2 multiply_reduce_fusion
  808.4 2.4 multiply_reduce_fusion.1
  811.6 62.5 %psum.15 = f32[8]{0:T(128)S(1)} all-reduce(f32[8]{0:T(128)S(1)} %pad_maximum_fusion.2), channel_id=1, replica_groups=mesh['data'=128] {'data'}, use_global_device_ids=true, to_apply=%region_11.0 | all-reduce | flops 8 | bytes 64 | tf_op jit(solution)/shard_map/psum | solution.py:75
  874.2 0.9 fusion.42
  875.1 0.8 fusion.41
  875.9 66.8 %all-gather.3.cloned.1.call-done = bf16[2,768,3072]{2,0,1:T(2,128)(2,1)} async-done(((bf16[2,6,3072]{2,0,1:T(2,128)(2,1)}), bf16[2,768,3072]{2,0,1:T(2,128)(2,1)}) %all-gather.3.cloned.1.call-update) | async-done | bytes 9437200 | tf_op jit(solution)/shard_map/all_gather | solution.py:79
  942.8 10.3 %copy.34 = bf16[2,768,3072]{2,1,0:T(8,128)(2,1)} copy(bf16[2,768,3072]{2,0,1:T(2,128)(2,1)} %all-gather.3.cloned.1.call-done) | data formatting | bytes 18874368
  953.1 60.6 %all-gather.5.cloned.1.call-done = bf16[2,3072,768]{2,1,0:T(8,128)(2,1)} async-done(((bf16[2,24,768]{2,1,0:T(8,128)(2,1)}), bf16[2,3072,768]{2,1,0:T(8,128)(2,1)}) %all-gather.5.cloned.1.call-update) | async-done | bytes 9437200 | tf_op jit(solution)/shard_map/all_gather | solution.py:80
  1013.7 8.1 copy.45
  (39 shorter events, 0.9 us)
Async XLA Ops:
  7.2 1.4 copy-start
  7.2 293.8 %all-reduce.5.cloned.1.call-start = ((), (), s32[]{:S(2)}) async-start(), calls=%async_computation.6 | async-start | bytes 37748736
  8.6 12.7 %copy-start.6 = (bf16[2,3072,768]{2,1,0:T(8,128)(2,1)S(1)}, bf16[2,3072,768]{2,1,0:T(8,128)(2,1)}, u32[]{:S(2)}) copy-start(bf16[2,3072,768]{2,1,0:T(8,128)(2,1)} %param.15) | copy-start | bytes 28311556
  8.6 17.8 %slice-start = ((s8[9437184]{0:T(1024)(128)(4,1)}), s8[4194304]{0:T(1024)(128)(4,1)S(1)}, s32[]{:S(2)}) async-start(s8[9437184]{0:T(1024)(128)(4,1)} %bitcast.50), calls=%async_computation.7 | async-start | bytes 8388608
  8.6 17.8 %slice-start.1 = ((s8[9437184]{0:T(1024)(128)(4,1)}), s8[4194304]{0:T(1024)(128)(4,1)S(1)}, s32[]{:S(2)}) async-start(s8[9437184]{0:T(1024)(128)(4,1)} %bitcast.50), calls=%async_computation.8 | async-start | bytes 8388608
  21.3 5.1 copy-start.8
  21.3 5.1 slice-start.2
  26.4 8.0 copy-start.7
  78.6 440.5 %reduce-scatter.7.cloned.1.call-start = ((), (), s32[]{:S(2)}) async-start(), calls=%async_computation.3 | async-start | bytes 9510912 | tf_op jit(solution)/shard_map/reduce_scatter | solution.py:59
  89.7 1.4 copy-start.9
  89.7 648.9 %reduce-scatter.5.cloned.1.call-start = ((), (), s32[]{:S(2)}) async-start(), calls=%async_computation.2 | async-start | bytes 9510912 | tf_op jit(solution)/shard_map/reduce_scatter | solution.py:59
  101.4 0.9 copy-start.5
  101.4 1.0 copy-start.2
  101.4 841.4 %all-gather.3.cloned.1.call-start = ((), (), s32[]{:S(2)}) async-start(), calls=%async_computation.4 | async-start | bytes 9510912 | tf_op jit(solution)/shard_map/all_gather | solution.py:79
  808.4 144.7 %copy-start.3 = (f32[2,24,768]{2,1,0:T(8,128)}, f32[2,24,768]{2,1,0:T(8,128)S(1)}, u32[]{:S(2)}) copy-start(f32[2,24,768]{2,1,0:T(8,128)S(1)} %get-tuple-element.60) | copy-start | bytes 442372
  808.4 144.7 %copy-start.4 = (f32[2,24,768]{2,1,0:T(8,128)}, f32[2,24,768]{2,1,0:T(8,128)S(1)}, u32[]{:S(2)}) copy-start(f32[2,24,768]{2,1,0:T(8,128)S(1)} %get-tuple-element.62) | copy-start | bytes 442372
  875.1 138.6 %all-gather.5.cloned.1.call-start = ((), (), s32[]{:S(2)}) async-start(), calls=%async_computation.5 | async-start | bytes 9510912 | tf_op jit(solution)/shard_map/all_gather | solution.py:80
  1013.7 8.2 copy-start.1
Sparse Core Ops, SparseCore 0:
  78.7 222.3 all-reduce.4
  306.0 213.0 reduce-scatter.6
  524.1 214.5 reduce-scatter.4
  875.2 67.5 all-gather.2
  945.8 67.8 all-gather.4
where the time goes:
time: 1030 us
  waiting for transfers between devices  757 us (73%)
  blocking collectives  127 us (12%)
  matrix products  91.2 us (9%)
  local copies, waits for them, and re-layouts  23 us (2%)
  between operations  18.4 us (2%)
  other arithmetic  12.8 us (1%)
    reduce_scatter x2, waiting for transfers between devices, reduce_rows(): lax.psum_scatter(grad, 'data', scatter_dimension=0, tiled=True) / group_size  431 us
    unnamed x6, waiting for transfers between devices  198 us
    all_gather x1, waiting for transfers between devices, device_step(): lax.all_gather(master_up_out.astype(jnp.bfloat16), 'data', axis=1, tiled=...  66.8 us
    psum x1, blocking collectives, device_step(): grad_norm = jnp.sqrt(lax.psum(local_sq, 'data'))  64.3 us
    psum x1, blocking collectives, device_step(): norm_stats = lax.psum(local_stats, 'data')  62.5 us
    all_gather x1, waiting for transfers between devices, device_step(): lax.all_gather(master_down_out.astype(jnp.bfloat16), 'data', axis=1, tile...  60.6 us
    unnamed x28, local copies, waits for them, and re-layouts  22 us
  transfers between devices with their start and end apart: 5, of which 5 were waited for; matrix products, arithmetic and copies ran while one was open for 4% of the time, Pallas kernels for 0%

commit v1 on v0

v1 whole, which is shorter than its diff:
```python
import functools
import math

import jax
import jax.numpy as jnp
from jax import lax
from jax.experimental import pallas as pl
from jax.experimental.pallas import tpu as pltpu
from jax.sharding import PartitionSpec as P

STEP = 10
BETA_ONE = 0.9
BETA_TWO = 0.95
ADAM_EPS = 1e-8
NORM_EPS = 1e-6
INV_SQRT_TWO = 0.7071067811865476
INV_SQRT_TWO_PI = 0.3989422804014327

MESH = pl.DeviceIdType.MESH
F32 = jnp.float32
BF16 = jnp.bfloat16


def gelu_parts(pre_act):
    normal_cdf = 0.5 * (1.0 + lax.erf(pre_act * INV_SQRT_TWO))
    normal_pdf = jnp.exp(-0.5 * pre_act * pre_act) * INV_SQRT_TWO_PI
    return pre_act * normal_cdf, normal_cdf + pre_act * normal_pdf


def local_grads(act_in, grad_out, w_up, w_down):
    z_one = jnp.einsum("td,df->tf", act_in, w_up[0], preferred_element_type=jnp.float32)
    gelu_one, slope_one = gelu_parts(z_one)
    act_one = gelu_one.astype(jnp.bfloat16)
    hidden = jnp.einsum("tf,fd->td", act_one, w_down[0], preferred_element_type=jnp.float32).astype(jnp.bfloat16)
    z_three = jnp.einsum("td,df->tf", hidden, w_up[1], preferred_element_type=jnp.float32)
    gelu_three, slope_three = gelu_parts(z_three)
    act_three = gelu_three.astype(jnp.bfloat16)
    g_four = jnp.einsum("tf,td->fd", act_three, grad_out, preferred_element_type=jnp.float32)
    dz_three = (jnp.einsum("td,fd->tf", grad_out, w_down[1], preferred_element_type=jnp.float32) * slope_three).astype(jnp.bfloat16)
    g_three = jnp.einsum("td,tf->df", hidden, dz_three, preferred_element_type=jnp.float32)
    d_hidden = jnp.einsum("tf,df->td", dz_three, w_up[1], preferred_element_type=jnp.float32).astype(jnp.bfloat16)
    g_two = jnp.einsum("tf,td->fd", act_one, d_hidden, preferred_element_type=jnp.float32)
    dz_one = (jnp.einsum("td,fd->tf", d_hidden, w_down[0], preferred_element_type=jnp.float32) * slope_one).astype(jnp.bfloat16)
    g_one = jnp.einsum("td,tf->df", act_in, dz_one, preferred_element_type=jnp.float32)
    return g_one, g_two, g_three, g_four


def adam_direction(exp_avg, exp_sq, grad, clip_scale):
    bias_one = 1.0 - BETA_ONE ** STEP
    bias_two = 1.0 - BETA_TWO ** STEP
    avg_new = BETA_ONE * exp_avg + (1.0 - BETA_ONE) * clip_scale * grad
    sq_new = BETA_TWO * exp_sq + (1.0 - BETA_TWO) * (clip_scale * clip_scale) * (grad * grad)
    direction = (avg_new / bias_one) / (jnp.sqrt(sq_new / bias_two) + ADAM_EPS)
    return avg_new, sq_new, direction


class Unit:
    def __init__(self, kind, k, off, cols, order):
        self.kind, self.k, self.off, self.cols, self.order = kind, k, off, cols, order
        self.dims = "zy" if kind == "up" else "zyx"
        self.shape = (4,) * len(self.dims) + (48, cols)

    def half(self, phase, dest, h, me):
        if self.kind == "up" and phase == 2:
            return (dest, h), (6, self.cols)
        fixed = {d: me[d] for d in self.order[:phase]}
        fixed[self.order[phase]] = dest
        index, shape, split = [], [], False
        for d in self.dims:
            if d in fixed:
                index.append(fixed[d])
            elif not split:
                index.append(pl.ds(2 * h, 2))
                shape.append(2)
                split = True
            else:
                index.append(slice(None))
                shape.append(4)
        if split:
            return tuple(index), tuple(shape) + (48, self.cols)
        return tuple(index) + (pl.ds(24 * h, 24),), (24, self.cols)

    def half_shape(self, phase):
        return self.half(phase, 0, 0, dict(x=0, y=0, z=0))[1]


def make_units(up_cols, down_cols):
    u, d = up_cols // 2, down_cols // 3
    return [
        Unit("down", 1, 0, 2 * d, "xyz"),
        Unit("up", 1, 0, u, "zyx"),
        Unit("up", 1, u, u, "yzx"),
        Unit("down", 1, 2 * d, d, "yxz"),
        Unit("down", 0, 0, 2 * d, "xzy"),
        Unit("down", 0, 2 * d, d, "zxy"),
        Unit("up", 0, 0, u, "zyx"),
        Unit("up", 0, u, u, "yzx"),
    ]


def event_order(units):
    rate, hop, pair_rate, add_rate = 46600.0, 2.5, 550000.0, 1500000.0
    link, now, pair = {}, 0.0, 2.0
    ready, state, events = [], [], []
    size = [math.prod(u.shape) * 4 for u in units]
    for b in size:
        pair += b / pair_rate
        ready.append(pair)
        state.append(0)

    def send(d, sign, start, nbytes):
        key = (d, sign)
        link[key] = max(link.get(key, 0.0), start) + nbytes / rate
        return link[key] + hop

    last = [[0.0, 0.0] for _ in units]
    while any(s < 8 for s in state):
        i = min((j for j in range(len(units)) if state[j] < 8), key=lambda j: (ready[j], j))
        u, s = units[i], state[i]
        events.append((i, s))
        now = max(now, ready[i])
        if s == 0:
            now += 3 * size[i] / add_rate
        elif s < 7:
            phase = (s - 1) // 2
            now += 0.2 + 3 * size[i] / 4 ** (phase + 1) / add_rate
        if s < 7:
            phase = s // 2 if s % 2 == 0 else (s - 1) // 2
            if phase < 3:
                b = math.prod(u.half_shape(phase)) * 4
                d = u.order[phase]
                if s % 2 == 0:
                    arrive = [send(d, g, now, b) for g in (1, -1)]
                    last[i] = [send(d, g, now, b) for g in (1, -1)]
                    ready[i] = max(arrive)
                else:
                    arrive = [send(d, g, now, b) for g in (1, -1)]
                    ready[i] = max(arrive)
            else:
                ready[i] = now + 2.0
        state[i] += 1
    return events


def position():
    me = lax.axis_index("data")
    return dict(z=me // 32, y=(me // 8) % 4, x=(me // 2) % 4, c=me % 2)


def device_of(at):
    return (((at["z"] * 4 + at["y"]) * 4 + at["x"]) * 2 + at["c"],)


def moved(me, d, by):
    return device_of({**me, d: (me[d] + by) % 4})


def partner_of(me):
    return device_of({**me, "c": 1 - me["c"]})


def group_peers(me):
    first, second = [], []
    j, q = me["x"] * 2 + me["c"], me["z"] * 4 + me["y"]
    for t in range(1, 8):
        o = (j + t) % 8
        first.append((o, device_of({**me, "x": o // 2, "c": o % 2})))
    for t in range(1, 16):
        o = (q + t) % 16
        second.append((o, device_of({**me, "z": o // 4, "y": o % 4})))
    return first, second


def remote(src, dst, send_sem, recv_sem, device):
    return pltpu.make_async_remote_copy(src_ref=src, dst_ref=dst, send_sem=send_sem, recv_sem=recv_sem, device_id=device, device_id_type=MESH)


def add_into(dst, *srcs):
    lead = dst.shape[:-2]
    if not lead:
        dst[...] = functools.reduce(lambda a, b: a + b, [s[...] for s in srcs], dst[...])
        return

    def body(i, carry):
        index = []
        for n in reversed(lead):
            index.append(i % n)
            i = i // n
        index = tuple(reversed(index))
        dst[index] = functools.reduce(lambda a, b: a + b, [s[index] for s in srcs], dst[index])
        return carry

    lax.fori_loop(0, math.prod(lead), body, 0)


def reduce_update_kernel(units, events, *refs):
    n_units = len(units)
    take = iter(refs)
    g_ref = {("up", 0): next(take), ("down", 0): next(take), ("up", 1): next(take), ("down", 1): next(take)}
    master = dict(up=next(take), down=next(take))
    avg = dict(up=next(take), down=next(take))
    sq = dict(up=next(take), down=next(take))
    rate_ref, clip_ref = next(take), next(take)
    weight = dict(up=next(take), down=next(take))
    master_out = dict(up=next(take), down=next(take))
    avg_out = dict(up=next(take), down=next(take))
    sq_out = dict(up=next(take), down=next(take))
    norm_ref = next(take)
    acc = [next(take) for _ in units]
    recv = [[[next(take) for _ in range(6)] for _ in range(3)] for _ in units]
    xbuf = {i: next(take) for i, u in enumerate(units) if u.kind == "up"}
    fin = [next(take) for _ in units]
    slots = {}
    slot_of = {}
    for i, u in enumerate(units):
        if (u.kind, u.cols, u.off) not in slots:
            slots[u.kind, u.cols, u.off] = next(take)
        slot_of[i] = slots[u.kind, u.cols, u.off]
    grad = dict(up=next(take), down=next(take))
    small_src, small_one, small_two = next(take), next(take), next(take)
    load_sem, pair_send, pair_recv, ring_send, ring_recv, fin_send, fin_recv = [next(take) for _ in range(7)]
    one_send, one_recv, two_send, two_recv = [next(take) for _ in range(4)]

    me = position()
    core = me["c"]
    partner = partner_of(me)
    first, second = group_peers(me)

    barrier = pltpu.get_barrier_semaphore()
    for _, device in first + second:
        pl.semaphore_signal(barrier, inc=1, device_id=device, device_id_type=MESH)
    pl.semaphore_wait(barrier, len(first) + len(second))

    def columns(u, c):
        ref = g_ref[u.kind, u.k]
        width = ref.shape[-1] // 2
        start = pl.multiple_of(c * width + u.off, 128)
        return ref.at[(slice(None),) * (len(ref.shape) - 1) + (pl.ds(start, u.cols),)]

    pair_copy = [remote(columns(u, 1 - core), acc[i], pair_send.at[i], pair_recv.at[i], partner) for i, u in enumerate(units)]
    load_copy = [pltpu.make_async_copy(columns(u, core), slot_of[i], load_sem.at[i]) for i, u in enumerate(units)]
    later = {}
    for i, u in enumerate(units):
        earlier = [j for j in range(i) if slot_of[j] is slot_of[i]]
        if earlier:
            later[earlier[-1]] = i
        else:
            load_copy[i].start()
        pair_copy[i].start()

    sent = []

    def ring(i, phase, n):
        u = units[i]
        d = u.order[phase]
        base = xbuf[i] if u.kind == "up" and phase == 2 else acc[i]
        by = 1 if n % 2 == 0 else -1
        dest = (me[d] + (2 if n < 2 else by)) % 4
        h = (0, 1, 1, 0, 0, 1)[n]
        src = base.at[u.half(phase, dest, h, me)[0]]
        s = (i * 3 + phase) * 6 + n
        return remote(src, recv[i][phase][n], ring_send.at[s], ring_recv.at[s], moved(me, d, by)), src

    def start_phase(i, phase):
        u = units[i]
        if u.kind == "up" and phase == 2:
            block = acc[i][me["z"], me["y"]]
            for p in range(8):
                xbuf[i][p // 2, p % 2] = block[6 * p:6 * p + 6]
        for n in range(4):
            copy, _ = ring(i, phase, n)
            copy.start()
            sent.append(copy)

    for i, s in events:
        u = units[i]
        if s == 0:
            load_copy[i].wait()
            pair_copy[i].wait_recv()
            add_into(acc[i], slot_of[i])
            if i in later:
                load_copy[later[i]].start()
            start_phase(i, 0)
        elif s < 7 and s % 2 == 1:
            phase = (s - 1) // 2
            for n in (4, 5):
                copy, src = ring(i, phase, n)
                ring(i, phase, n - 4)[0].wait_recv()
                add_into(src, recv[i][phase][n - 4])
                copy.start()
                sent.append(copy)
        elif s < 7:
            phase = s // 2 - 1
            d = u.order[phase]
            base = xbuf[i] if u.kind == "up" and phase == 2 else acc[i]
            for n in (2, 3, 4, 5):
                ring(i, phase, n)[0].wait_recv()
            for h, (a, b) in enumerate(((4, 3), (2, 5))):
                add_into(base.at[u.half(phase, me[d], h, me)[0]], recv[i][phase][a], recv[i][phase][b])
            if phase < 2:
                start_phase(i, phase + 1)
            else:
                src = xbuf[i].at[me["x"], 1 - core] if u.kind == "up" else acc[i].at[me["z"], me["y"], me["x"], pl.ds(pl.multiple_of(24 * (1 - core), 8), 24)]
                copy = remote(src, fin[i], fin_send.at[i], fin_recv.at[i], partner)
                copy.start()
                sent.append(copy)
        else:
            src = xbuf[i].at[me["x"], core] if u.kind == "up" else acc[i].at[me["z"], me["y"], me["x"], pl.ds(pl.multiple_of(24 * core, 8), 24)]
            remote(src, fin[i], fin_send.at[i], fin_recv.at[i], partner).wait_recv()
            own, other = src[...], fin[i][...]
            half = grad[u.kind].shape[-1] // 2
            grad[u.kind][u.k, :, u.off:u.off + u.cols] = jnp.where(core == 0, own, other) * (1.0 / 128.0)
            grad[u.kind][u.k, :, half + u.off:half + u.off + u.cols] = jnp.where(core == 0, other, own) * (1.0 / 128.0)

    def total(values):
        row = lax.broadcasted_iota(jnp.int32, (8, 128), 0)
        tile = jnp.zeros((8, 128), F32)
        for r, value in enumerate(values):
            tile = jnp.where(row == r, value, tile)
        return tile

    def all_sum(at, tile):
        for stage, (peers, own, buf, send, recv_s) in enumerate((
            (first, me["x"] * 2 + core, small_one, one_send, one_recv),
            (second, me["z"] * 4 + me["y"], small_two, two_send, two_recv),
        )):
            small_src[at, stage] = tile
            buf[at, own] = tile
            for t, (o, device) in enumerate(peers):
                copy = remote(small_src.at[at, stage], buf.at[at, own], send.at[at, t], recv_s.at[at, own], device)
                copy.start()
                sent.append(copy)
            for o, device in peers:
                remote(small_src.at[at, stage], buf.at[at, o], send.at[at, 0], recv_s.at[at, o], device).wait_recv()
            tile = buf[at, 0]
            for o in range(1, len(peers) + 1):
                tile = tile + buf[at, o]
        return tile

    def squares(x):
        return jnp.sum(x * x)

    keys = (("up", 0), ("down", 0), ("up", 1), ("down", 1))
    local_sq = functools.reduce(lambda a, b: a + b, [squares(grad[kind][k]) for kind, k in keys])
    sums = all_sum(0, total([local_sq] + [squares(master[kind][k]) for kind, k in keys]))
    norm = jnp.sqrt(sums[0:1, :])
    norm_ref[...] = jnp.broadcast_to(norm, norm_ref.shape)
    clip_scale = jnp.minimum(1.0, clip_ref[0] / (norm + NORM_EPS))[:, 0:1]
    master_norm = jnp.sqrt(sums)
    local = []
    for kind, k in keys:
        avg_new, sq_new, direction = adam_direction(avg[kind][k], sq[kind][k], grad[kind][k], clip_scale)
        avg_out[kind][k] = avg_new
        sq_out[kind][k] = sq_new
        grad[kind][k] = direction
        local.append(squares(direction))
    dir_norm = jnp.sqrt(all_sum(1, total(local)))
    for r, (kind, k) in enumerate(keys):
        ratio = (master_norm[r + 1:r + 2, :] / dir_norm[r:r + 1, :])[:, 0:1]
        new = master[kind][k] - rate_ref[0] * ratio * grad[kind][k]
        master_out[kind][k] = new
        weight[kind][k] = new.astype(BF16)

    for copy in pair_copy + sent:
        copy.wait_send()


def reduce_update(grads, master, avg, sq, learn_rate, clip_norm):
    up_cols, down_cols = grads[0].shape[1], grads[1].shape[1]
    units = make_units(up_cols // 2, down_cols // 2)
    events = event_order(units)
    views = [g.reshape((4, 4, 48, up_cols)) if i % 2 == 0 else g.reshape((4, 4, 4, 48, down_cols)) for i, g in enumerate(grads)]
    scratch = [pltpu.VMEM(u.shape, F32) for u in units]
    scratch += [pltpu.VMEM(u.half_shape(p), F32) for u in units for p in range(3) for _ in range(6)]
    scratch += [pltpu.VMEM((4, 2, 6, u.cols), F32) for u in units if u.kind == "up"]
    scratch += [pltpu.VMEM((6 if u.kind == "up" else 24, u.cols), F32) for u in units]
    seen = set()
    for u in units:
        if (u.kind, u.cols, u.off) not in seen:
            seen.add((u.kind, u.cols, u.off))
            scratch.append(pltpu.VMEM(u.shape, F32))
    scratch += [pltpu.VMEM(master[0].shape, F32), pltpu.VMEM(master[1].shape, F32)]
    scratch += [pltpu.VMEM((2, 2, 8, 128), F32), pltpu.VMEM((2, 8, 8, 128), F32), pltpu.VMEM((2, 16, 8, 128), F32)]
    n = len(units)
    dma = pltpu.SemaphoreType.DMA
    scratch += [dma((n,)), dma((n,)), dma((n,)), dma((n * 18,)), dma((n * 18,)), dma((n,)), dma((n,))]
    scratch += [dma((2, 7)), dma((2, 8)), dma((2, 15)), dma((2, 16))]
    vmem, smem = pl.BlockSpec(memory_space=pltpu.VMEM), pl.BlockSpec(memory_space=pltpu.SMEM)
    state = [jax.ShapeDtypeStruct(a.shape, F32) for a in master]
    outs = pl.pallas_call(
        functools.partial(reduce_update_kernel, units, events),
        out_shape=[jax.ShapeDtypeStruct(a.shape, BF16) for a in master] + state * 3 + [jax.ShapeDtypeStruct((8, 128), F32)],
        in_specs=[pl.BlockSpec(memory_space=pl.ANY)] * 4 + [vmem] * 6 + [smem] * 2,
        out_specs=[vmem] * 9,
        scratch_shapes=scratch,
        compiler_params=pltpu.CompilerParams(collective_id=0, has_side_effects=True, vmem_limit_bytes=60 * 1024 * 1024),
        name="reduce_update",
    )(*views, *master, *avg, *sq, learn_rate.reshape(1), clip_norm.reshape(1))
    return outs


def solution(mesh):
    batch_rows = P("data", None)
    state_rows = P(None, "data", None)
    replicated = P()

    def device_step(act_in, grad_out, w_up, w_down, master_up, master_down, exp_avg_up, exp_avg_down, exp_sq_up, exp_sq_down, learn_rate, clip_norm):
        grads = local_grads(act_in, grad_out, w_up, w_down)
        outs = reduce_update(grads, (master_up, master_down), (exp_avg_up, exp_avg_down), (exp_sq_up, exp_sq_down), learn_rate, clip_norm)
        block_up, block_down, master_up_out, master_down_out, avg_up, avg_down, sq_up, sq_down, norm = outs
        new_w_up = lax.all_gather(block_up, "data", axis=1, tiled=True)
        new_w_down = lax.all_gather(block_down, "data", axis=1, tiled=True)
        return (new_w_up, new_w_down, master_up_out, master_down_out, avg_up, avg_down, sq_up, sq_down, norm[0, 0])

    return jax.shard_map(device_step, mesh=mesh, in_specs=(batch_rows, batch_rows, replicated, replicated, state_rows, state_rows, state_rows, state_rows, state_rows, state_rows, replicated, replicated), out_specs=(replicated, replicated, state_rows, state_rows, state_rows, state_rows, state_rows, state_rows, replicated), check_vma=False)
```

time: 1030 us -> 391 us (0.38)
  waiting for transfers between devices: 757 us -> 123 us
  blocking collectives: 127 us -> 0 us
  Pallas kernels: 0 us -> 121 us
  other arithmetic: 12.8 us -> 0.01 us
  local copies, waits for them, and re-layouts: 23 us -> 35.7 us
    reduce_scatter x2 -> x0, waiting for transfers between devices: 431 us -> none  [reduce_rows(): lax.psum_scatter(grad, 'data', scatter_dimension=0, tiled=True) / group_size]
    unnamed x6 -> x2, waiting for transfers between devices: 198 us -> 0.71 us
    psum x2 -> x0, blocking collectives: 127 us -> none  [the longest x1 64.3 us: device_step(): grad_norm = jnp.sqrt(lax.psum(local_sq, 'data'))]
    pallas_call x0 -> x1, Pallas kernels: none -> 121 us  [reduce_update(): pl.pallas_call(functools.partial(reduce_update_kernel, units, events), ou...]
    unnamed x28 -> x45, local copies, waits for them, and re-layouts: 22 us -> 32.9 us
  transfers between devices with their start and end apart: 5 -> 2, of which waited for: 5 -> 2; matrix products, arithmetic and copies ran while one was open for 4% -> 4% of each run, Pallas kernels for 0% -> 0%
where the time goes in v1:
time: 391 us; the launch traced here: 390 us
  waiting for transfers between devices  123 us (31%)
  Pallas kernels  121 us (31%)
  matrix products  95.1 us (24%)
  local copies, waits for them, and re-layouts  35.7 us (9%)
  between operations  15.4 us (4%)
    pallas_call x1, Pallas kernels, reduce_update(): pl.pallas_call(functools.partial(reduce_update_kernel, units, events), ou...  121 us
    all_gather x1, waiting for transfers between devices, device_step(): new_w_up = lax.all_gather(block_up, 'data', axis=1, tiled=True)  61.6 us
    all_gather x1, waiting for transfers between devices, device_step(): new_w_down = lax.all_gather(block_down, 'data', axis=1, tiled=True)  60.8 us
    unnamed x45, local copies, waits for them, and re-layouts  32.9 us
    dot_general x1, matrix products, local_grads(): jnp.einsum('td,tf->df', act_in, dz_one, preferred_element_type=jnp.float32)  16.5 us
    dot_general x1, matrix products, local_grads(): jnp.einsum('tf,td->fd', act_three, grad_out, preferred_element_type=jnp.f...  13.4 us
    dot_general x1, matrix products, local_grads(): jnp.einsum('td,df->tf', act_in, w_up[0], preferred_element_type=jnp.float32)  12.8 us
    dot_general x1, matrix products, local_grads(): jnp.einsum('td,fd->tf', grad_out, w_down[1], preferred_element_type=jnp.f...  12.2 us
  transfers between devices with their start and end apart: 2, of which 2 were waited for; matrix products, arithmetic and copies ran while one was open for 4% of the time, Pallas kernels for 0%

profile of v1, /device:TPU:1, one launch (start us, length us, event | category | flops | bytes accessed | tf_op | source)
XLA Modules:
  0.0 390.2 jit_solution(560017546257992634)
XLA Ops:
  7.2 0.0 all-gather.3.cloned.1.call-start
  7.2 1.4 copy-done
  8.6 12.8 %multiply_convert_fusion.1 = (bf16[1024,3072]{1,0:T(8,128)(2,1)S(1)}, f32[1024,3072]{1,0:T(8,128)}) fusion(bf16[1024,768]{1,0:T(8,128)(2,1)S(1)} %copy-done, bf16[2,768,3072]{2,1,0:T(8,128)(2,1)} %param.14), kind=kOutput, calls=%fused_computation.16 | convolution fusion | flops 4847566848 | bytes 25165824 | tf_op jit(solution)/shard_map/td,df->tf/dot_general | solution.py:31
  21.4 2.7 copy-done.12
  24.1 5.0 %fusion.29 = bf16[1024,768]{1,0:T(8,128)(2,1)S(1)} fusion(bf16[1024,3072]{1,0:T(8,128)(2,1)S(1)} %get-tuple-element.45, bf16[2,3072,768]{2,1,0:T(8,128)(2,1)S(1)} %copy-done.7), kind=kOutput, calls=%fused_computation.35 | convolution fusion | flops 4832624640 | bytes 12582912 | tf_op jit(solution)/shard_map/tf,fd->td/dot_general | solution.py:34
  29.2 1.1 copy-done.10
  30.3 7.9 %fusion.15 = f32[1024,3072]{1,0:T(8,128)} fusion(bf16[1024,768]{1,0:T(8,128)(2,1)S(1)} %fusion.29, bf16[2,768,3072]{2,1,0:T(8,128)(2,1)S(1)} %bitcast.52), kind=kOutput, calls=%fused_computation.21 | convolution fusion | flops 4831838208 | bytes 18874368 | tf_op jit(solution)/shard_map/td,df->tf/dot_general | solution.py:35
  38.2 12.2 %fusion.5 = bf16[1024,3072]{1,0:T(8,128)(2,1)S(1)} fusion(f32[1024,3072]{1,0:T(8,128)} %fusion.15, bf16[1024,768]{1,0:T(8,128)(2,1)S(1)} %copy-done.8, bf16[2,3072,768]{2,1,0:T(8,128)(2,1)S(1)} %copy-done.7), kind=kOutput, calls=%fused_computation.7 | convolution fusion | flops 4863295488 | bytes 25165824 | tf_op jit(solution)/shard_map/td,fd->tf/dot_general | solution.py:39
  50.4 13.4 %fusion.12 = f32[3072,768]{1,0:T(8,128)} fusion(bf16[1024,768]{1,0:T(8,128)(2,1)S(1)} %copy-done.8, f32[1024,3072]{1,0:T(8,128)} %fusion.15), kind=kOutput, calls=%fused_computation.18 | convolution fusion | flops 4847566848 | bytes 23592960 | tf_op jit(solution)/shard_map/tf,td->fd/dot_general | solution.py:38
  63.8 6.2 %fusion.32 = bf16[1024,768]{1,0:T(8,128)(2,1)} fusion(bf16[1024,3072]{1,0:T(8,128)(2,1)S(1)} %fusion.5, bf16[2,768,3072]{2,1,0:T(8,128)(2,1)S(1)} %bitcast.52), kind=kOutput, calls=%fused_computation.36 | convolution fusion | flops 4832624640 | bytes 12582912 | tf_op jit(solution)/shard_map/tf,df->td/dot_general | solution.py:41
  70.1 10.4 %fusion.41 = f32[768,3072]{1,0:T(8,128)} fusion(bf16[1024,768]{1,0:T(8,128)(2,1)S(1)} %copy-done.11, bf16[1024,3072]{1,0:T(8,128)(2,1)} %copy-done.9), kind=kOutput, calls=%fused_computation.41 | convolution fusion | flops 4831838208 | bytes 17301504 | tf_op jit(solution)/shard_map/td,tf->df/dot_general | solution.py:40
  81.8 0.7 copy.27.refs_4_
  82.5 0.7 copy.28.refs_6_
  83.2 0.7 copy.29.refs_8_
  84.0 10.7 %fusion.40 = f32[3072,768]{1,0:T(8,128)} fusion(bf16[1024,3072]{1,0:T(8,128)(2,1)} %copy-done.12, bf16[1024,768]{1,0:T(8,128)(2,1)} %fusion.32), kind=kOutput, calls=%fused_computation.40 | convolution fusion | flops 4831838208 | bytes 17301504 | tf_op jit(solution)/shard_map/tf,td->fd/dot_general | solution.py:42
  94.7 16.5 %fusion.36 = f32[3072,768]{0,1:T(8,128)} fusion(bf16[1024,768]{1,0:T(8,128)(2,1)S(1)} %copy-done, f32[1024,3072]{1,0:T(8,128)} %get-tuple-element.46, bf16[1024,768]{1,0:T(8,128)(2,1)S(1)} %copy-done.13, bf16[2,3072,768]{2,1,0:T(8,128)(2,1)} %param.15), kind=kOutput, calls=%fused_computation.37 | convolution fusion | flops 9695133696 | bytes 29884416 | tf_op jit(solution)/shard_map/td,tf->df/dot_general | solution.py:44
  111.1 120.7 %reduce_update.1 = (bf16[2,6,3072]{2,1,0:T(8,128)(2,1)}, bf16[2,24,768]{2,1,0:T(8,128)(2,1)}, f32[2,6,3072]{2,1,0:T(8,128)}, f32[2,24,768]{2,1,0:T(8,128)}, f32[...) custom-call(f32[4,4,48,3072]{3,2,1,0:T(8,128)} %bitcast.50, ...), custom_call_target="tpu_custom_call" | custom-call | tf_op jit(solution)/shard_map/reduce_update/pallas_call | solution.py:390
  231.9 1.6 copy.30
  233.5 0.0 all-gather.3.cloned.1.call-update
  233.5 0.0 all-gather.5.cloned.1.call-start
  233.6 0.7 all-gather.5.cloned.1.call-update
  234.3 1.2 slice.21
  235.4 1.7 copy.32
  237.1 1.7 copy.33
  238.9 1.7 copy.34
  240.6 61.6 %all-gather.3.cloned.1.call-done = bf16[2,768,3072]{2,0,1:T(2,128)(2,1)} async-done(((bf16[2,6,3072]{2,0,1:T(2,128)(2,1)}), bf16[2,768,3072]{2,0,1:T(2,128)(2,1)}) %all-gather.3.cloned.1.call-update) | async-done | bytes 9437200 | tf_op jit(solution)/shard_map/all_gather | solution.py:411
  302.2 10.3 %copy.31 = bf16[2,768,3072]{2,1,0:T(8,128)(2,1)} copy(bf16[2,768,3072]{2,0,1:T(2,128)(2,1)} %all-gather.3.cloned.1.call-done) | data formatting | bytes 18874368
  312.5 60.8 %all-gather.5.cloned.1.call-done = bf16[2,3072,768]{2,1,0:T(8,128)(2,1)} async-done(((bf16[2,24,768]{2,1,0:T(8,128)(2,1)}), bf16[2,3072,768]{2,1,0:T(8,128)(2,1)}) %all-gather.5.cloned.1.call-update) | async-done | bytes 9437200 | tf_op jit(solution)/shard_map/all_gather | solution.py:412
  373.3 8.1 %copy.41 = bf16[2,3072,768]{2,1,0:T(8,128)(2,1)} copy(bf16[2,3072,768]{2,1,0:T(8,128)(2,1)} %all-gather.5.cloned.1.call-done) | data formatting | bytes 18874368
  381.4 0.7 copy.42
  382.0 0.7 copy.43
  382.7 0.7 copy.44
  (32 shorter events, 0.1 us)
Async XLA Ops:
  7.2 1.4 copy-start
  7.2 295.0 %all-gather.3.cloned.1.call-start = ((), (), s32[]{:S(2)}) async-start(), calls=%async_computation | async-start | bytes 9510912 | tf_op jit(solution)/shard_map/all_gather | solution.py:411
  8.6 15.5 %copy-start.7 = (bf16[2,3072,768]{2,1,0:T(8,128)(2,1)S(1)}, bf16[2,3072,768]{2,1,0:T(8,128)(2,1)}, u32[]{:S(2)}) copy-start(bf16[2,3072,768]{2,1,0:T(8,128)(2,1)} %param.15) | copy-start | bytes 28311556
  8.6 21.7 %slice-start = ((s8[9437184]{0:T(1024)(128)(4,1)}), s8[4194304]{0:T(1024)(128)(4,1)S(1)}, s32[]{:S(2)}) async-start(s8[9437184]{0:T(1024)(128)(4,1)} %bitcast.51), calls=%async_computation.2 | async-start | bytes 8388608
  8.6 21.7 %slice-start.1 = ((s8[9437184]{0:T(1024)(128)(4,1)}), s8[4194304]{0:T(1024)(128)(4,1)S(1)}, s32[]{:S(2)}) async-start(s8[9437184]{0:T(1024)(128)(4,1)} %bitcast.51), calls=%async_computation.3 | async-start | bytes 8388608
  21.4 2.7 copy-start.12
  24.1 6.2 %slice-start.2 = ((s8[9437184]{0:T(1024)(128)(4,1)}), s8[1048576]{0:T(1024)(128)(4,1)S(1)}, s32[]{:S(2)}) async-start(s8[9437184]{0:T(1024)(128)(4,1)} %bitcast.51), calls=%async_computation.4 | async-start | bytes 2097152
  29.1 1.1 copy-start.10
  30.3 7.9 %copy-start.8 = (bf16[1024,768]{1,0:T(8,128)(2,1)S(1)}, bf16[1024,768]{1,0:T(8,128)(2,1)}, u32[]{:S(2)}) copy-start(bf16[1024,768]{1,0:T(8,128)(2,1)} %param.13) | copy-start | bytes 4718596
  50.4 13.4 %copy-start.9 = (bf16[1024,3072]{1,0:T(8,128)(2,1)}, bf16[1024,3072]{1,0:T(8,128)(2,1)S(1)}, u32[]{:S(2)}) copy-start(bf16[1024,3072]{1,0:T(8,128)(2,1)S(1)} %fusion.5) | copy-start | bytes 18874372
  63.8 6.2 %copy-start.11 = (bf16[1024,768]{1,0:T(8,128)(2,1)S(1)}, bf16[1024,768]{1,0:T(8,128)(2,1)}, u32[]{:S(2)}) copy-start(bf16[1024,768]{1,0:T(8,128)(2,1)} %copy-done.10) | copy-start | bytes 4718596
  70.0 11.7 %copy-start.4 = (f32[2,6,3072]{2,0,1:T(2,128)S(1)}, f32[2,6,3072]{2,0,1:T(2,128)}, u32[]{:S(2)}) copy-start(f32[2,6,3072]{2,0,1:T(2,128)} %param.16) | copy-start | bytes 442372
  70.1 12.5 %copy-start.5 = (f32[2,6,3072]{2,0,1:T(2,128)S(1)}, f32[2,6,3072]{2,0,1:T(2,128)}, u32[]{:S(2)}) copy-start(f32[2,6,3072]{2,0,1:T(2,128)} %param.18) | copy-start | bytes 442372
  70.1 13.2 %copy-start.6 = (f32[2,6,3072]{2,0,1:T(2,128)S(1)}, f32[2,6,3072]{2,0,1:T(2,128)}, u32[]{:S(2)}) copy-start(f32[2,6,3072]{2,0,1:T(2,128)} %param.20) | copy-start | bytes 442372
  84.0 10.7 %copy-start.13 = (bf16[1024,768]{1,0:T(8,128)(2,1)S(1)}, bf16[1024,768]{1,0:T(8,128)(2,1)}, u32[]{:S(2)}) copy-start(bf16[1024,768]{1,0:T(8,128)(2,1)} %fusion.32) | copy-start | bytes 4718596
  233.5 139.8 %all-gather.5.cloned.1.call-start = ((), (), s32[]{:S(2)}) async-start(), calls=%async_computation.1 | async-start | bytes 9510912 | tf_op jit(solution)/shard_map/all_gather | solution.py:412
  373.3 8.1 %copy-start.3 = (f32[2,24,768]{2,1,0:T(8,128)S(1)}, f32[2,24,768]{2,1,0:T(8,128)}, u32[]{:S(2)}) copy-start(f32[2,24,768]{2,1,0:T(8,128)} %get-tuple-element.59) | copy-start | bytes 442372
  373.3 8.8 %copy-start.2 = (f32[2,24,768]{2,1,0:T(8,128)S(1)}, f32[2,24,768]{2,1,0:T(8,128)}, u32[]{:S(2)}) copy-start(f32[2,24,768]{2,1,0:T(8,128)} %get-tuple-element.61) | copy-start | bytes 442372
  373.3 9.4 %copy-start.1 = (f32[2,24,768]{2,1,0:T(8,128)S(1)}, f32[2,24,768]{2,1,0:T(8,128)}, u32[]{:S(2)}) copy-start(f32[2,24,768]{2,1,0:T(8,128)} %get-tuple-element.63) | copy-start | bytes 442372
Sparse Core Ops, SparseCore 0:
  233.6 68.5 all-gather.2
  305.3 67.8 all-gather.4
